TPU v7x, 256 devices: a whole 4x4x8 slice. The times are simulated.
256 devices in a mesh: dp: 32 (over z, x_hi, core), expert: 8 (over x_lo, y).
Axes of the slice: x: 4 (x_hi: 2, x_lo: 2; x = x_hi * 2 + x_lo), y: 4, z: 8, core: 2. Of those that a mesh axis runs over, the one named last changes fastest.
Arguments:
- x_rows: bfloat16 [131072, 1024], P(('dp', 'expert')), may hold values from -24 to 24
- dy_rows: bfloat16 [131072, 2048], P(('dp', 'expert')), may hold values from -0.0234375 to 0.0234375
- seg_blocks: int32 [256, 8], replicated, may hold values from 0 to 2, as said below
Outputs:
- expert_grad: float32 [8, 1024, 2048], P(None, 'dp', 'expert')
Inputs may be any that keep to these rules, and one draw needn't show every extreme that they name: `seg_blocks`: on every device the entries sum to at most 4; one expert has exactly 2 blocks on every device.
All inputs are finite; a program needn't handle non-finite values.
Results may differ from a plain program's by a relative error of at most 0.0003.
Values may be sent and summed in bfloat16 or wider, within the bound.
A program may use at most 128 MiB of HBM per device.

v0:
```python
import jax
import jax.numpy as jnp
from jax import lax
from jax.sharding import PartitionSpec as P

BLOCK = 128
CAP = 2


def contract(left, right):
    return lax.dot_general(
        left, right, (((0,), (0,)), ((), ())), preferred_element_type=jnp.float32
    )


def shards(x_rows, dy_rows, seg_blocks):
    rows, hid = x_rows.shape
    ffn = dy_rows.shape[1]
    n_exp = lax.axis_size("expert")
    n_dp = lax.axis_size("dp")
    experts = seg_blocks.shape[1]
    nblk = rows // BLOCK
    device = lax.axis_index(("dp", "expert"))
    counts = lax.dynamic_slice(seg_blocks, (device, 0), (1, experts))[0]
    starts = jnp.cumsum(counts) - counts
    slots = jnp.arange(CAP, dtype=jnp.int32)
    live = slots[None, :] < counts[:, None]
    index = jnp.where(live, starts[:, None] + slots[None, :], 0).reshape(-1)
    keep = live.reshape(-1)[:, None, None]
    xsend = jnp.where(keep, x_rows.reshape(nblk, BLOCK, hid)[index], jnp.zeros((), x_rows.dtype))
    dysend = jnp.where(keep, dy_rows.reshape(nblk, BLOCK, ffn)[index], jnp.zeros((), dy_rows.dtype))
    xsend = xsend.reshape(experts, CAP * BLOCK, hid)
    dysend = dysend.reshape(experts, CAP * BLOCK, ffn)
    got_x, got_dy = (
        lax.all_to_all(xsend, "expert", split_axis=0, concat_axis=0, tiled=True),
        lax.all_to_all(dysend, "expert", split_axis=0, concat_axis=0, tiled=True),
    )
    got_x = got_x.reshape(n_exp * CAP * BLOCK, hid)
    got_dy = got_dy.reshape(n_exp * CAP * BLOCK, ffn)
    summed = lax.psum_scatter(contract(got_x, got_dy), "dp", scatter_dimension=0, tiled=True)
    return lax.all_to_all(
        summed.reshape(1, hid // n_dp, ffn), "expert", split_axis=2, concat_axis=0, tiled=True
    )


def solution(mesh):
    in_specs = (P(("dp", "expert"), None), P(("dp", "expert"), None), P())
    out_specs = P(None, "dp", "expert")
    return jax.shard_map(shards, mesh=mesh, in_specs=in_specs, out_specs=out_specs, check_vma=False)
```

profile of v0, /device:TPU:2, one launch (start us, length us, event | category | flops | bytes accessed | tf_op | source)
XLA Modules:
  0.0 380.6 jit_solution(2443288582051426192)
XLA Ops:
  6.5 0.0 copy-start
  6.5 1.0 dynamic-slice_reduce_fusion
  7.6 0.1 iota_compare_fusion
  7.6 0.2 reduce-window.8
  7.8 0.1 add_select_fusion
  7.9 0.1 select_n.41
  8.0 0.1 copy.9
  8.1 0.1 broadcast_bitcast_fusion
  8.2 4.0 %gather_fusion = bf16[16,128,1024]{2,1,0:T(8,128)(2,1)} fusion(bf16[4,128,1024]{2,1,0:T(8,128)(2,1)} %bitcast.27, s32[1024]{0:T(1024)S(1)} %pad_clamp_fusion), kind=kCustom, calls=%fused_computation | custom fusion | bytes 8388672 | tf_op jit(solution)/shard_map/gather | solution.py:30
  12.1 6.5 %copy.10 = bf16[8,256,1024]{1,2,0:T(8,128)(2,1)} copy(bf16[8,256,1024]{2,1,0:T(8,128)(2,1)} %bitcast.26) | data formatting | bytes 8388608 | tf_op jit(solution)/shard_map/gather | solution.py:30
  18.6 4.4 %broadcast_select_fusion = bf16[8,256,1024]{1,2,0:T(8,128)(2,1)} fusion(bf16[8,256,1024]{1,2,0:T(8,128)(2,1)} %copy.10, pred[8,256]{1,0:T(8,128)(4,1)S(1)} %broadcast_bitcast_fusion), kind=kLoop, calls=%fused_computation.4 | loop fusion | flops 2097152 | bytes 8390656 | tf_op jit(solution)/shard_map/jit(_where)/select_n | solution.py:30
  23.0 6.7 %all-to-all-start = ((bf16[8,256,1024]{1,2,0:T(8,128)(2,1)}), bf16[8,256,1024]{1,2,0:T(8,128)(2,1)}, u32[]{:S(2)}, u32[]{:S(2)}) async-start(bf16[8,256,1024]{1,2,0:T(8,128)(2,1)} %broadcast_select_fusion), calls=%async_computation | async-start | bytes 8388608 | tf_op jit(solution)/shard_map/all_to_all | solution.py:35
  29.7 0.0 reduce-scatter.2.cloned.1.call-start
  29.7 0.0 copy-done
  29.7 4.6 %gather_fusion.1 = bf16[16,128,2048]{2,1,0:T(8,128)(2,1)} fusion(bf16[4,128,2048]{2,1,0:T(8,128)(2,1)S(1)} %bitcast.24, s32[1024]{0:T(1024)S(1)} %pad_clamp_fusion), kind=kCustom, calls=%fused_computation.1 | custom fusion | bytes 16777280 | tf_op jit(solution)/shard_map/gather | solution.py:31
  34.3 7.3 %bitcast_select_fusion = bf16[8,256,2048]{2,1,0:T(8,128)(2,1)} fusion(pred[8,256]{1,0:T(8,128)(4,1)S(1)} %broadcast_bitcast_fusion, bf16[8,256,2048]{2,1,0:T(8,128)(2,1)} %bitcast.25), kind=kLoop, calls=%fused_computation.2 | loop fusion | flops 4194304 | bytes 16779264 | tf_op jit(solution)/shard_map/jit(_where)/select_n | solution.py:31
  41.6 35.5 %all-to-all-done = bf16[8,256,1024]{1,2,0:T(8,128)(2,1)} async-done(((bf16[8,256,1024]{1,2,0:T(8,128)(2,1)}), bf16[8,256,1024]{1,2,0:T(8,128)(2,1)}, u32[]{:S(2)}, u32[]{:S(2)}) %all-to-all-start) | async-done | bytes 4194336 | tf_op jit(solution)/shard_map/all_to_all | solution.py:35
  77.0 98.7 %all_to_all.28 = bf16[8,256,2048]{2,1,0:T(8,128)(2,1)S(1)} all-to-all(bf16[8,256,2048]{2,1,0:T(8,128)(2,1)} %bitcast_select_fusion), channel_id=1, replica_groups=mesh['dp'=32,'expert'=8] {'expert'}, dimensions={0} | all-to-all | bytes 16777216 | tf_op jit(solution)/shard_map/all_to_all | solution.py:36
  175.7 12.7 %convolution_bitcast_fusion = f32[1024,2048]{1,0:T(8,128)} fusion(bf16[8,256,1024]{1,2,0:T(8,128)(2,1)} %all-to-all-done, bf16[8,256,2048]{2,1,0:T(8,128)(2,1)S(1)} %all_to_all.28), kind=kOutput, calls=%fused_computation.3 | convolution fusion | flops 8589934592 | bytes 20971520 | tf_op jit(solution)/shard_map/dot_general | solution.py:11
  188.5 0.0 reduce-scatter.2.cloned.1.call-update
  188.5 155.2 %reduce-scatter.2.cloned.1.call-done = f32[32,2048]{1,0:T(8,128)} async-done(((f32[1024,2048]{1,0:T(8,128)}), f32[32,2048]{1,0:T(8,128)}) %reduce-scatter.2.cloned.1.call-update) | async-done | bytes 262160 | tf_op jit(solution)/shard_map/reduce_scatter | solution.py:40
  343.7 2.1 copy.11
  345.8 0.5 broadcast.54
  346.3 10.3 %reduce.3 = f32[2048,32]{1,0:T(8,128)} reduce(f32[2048,1,32]{2,1,0:T(1,128)S(1)} %bitcast.28, f32[]{:T(128)} %broadcast.54), dimensions={1}, to_apply=%bitcast.19.reduce_sub_computation | reduce | bytes 524292
  356.7 1.7 reshape.143
  358.3 11.3 %all_to_all.29 = f32[8,1,8192]{2,1,0:T(1,128)S(1)} all-to-all(f32[8,1,8192]{2,1,0:T(1,128)S(1)} %reshape.143), channel_id=1, replica_groups=mesh['dp'=32,'expert'=8] {'expert'}, dimensions={0} | all-to-all | bytes 524288 | tf_op jit(solution)/shard_map/all_to_all | solution.py:41
  369.7 1.3 reduce.4
  370.9 1.8 reshape.144
  372.8 1.0 copy.12
  (3 shorter events, 0.0 us)
Async XLA Ops:
  6.5 23.2 %copy-start = (bf16[512,2048]{1,0:T(8,128)(2,1)S(1)}, bf16[512,2048]{1,0:T(8,128)(2,1)}, u32[]{:S(2)}) copy-start(bf16[512,2048]{1,0:T(8,128)(2,1)} %param.4) | copy-start | bytes 6291460
  23.0 54.0 %all-to-all-start = ((bf16[8,256,1024]{1,2,0:T(8,128)(2,1)}), bf16[8,256,1024]{1,2,0:T(8,128)(2,1)}, u32[]{:S(2)}, u32[]{:S(2)}) async-start(bf16[8,256,1024]{1,2,0:T(8,128)(2,1)} %broadcast_select_fusion), calls=%async_computation | async-start | bytes 8388608 | tf_op jit(solution)/shard_map/all_to_all | solution.py:35
  29.7 314.0 %reduce-scatter.2.cloned.1.call-start = ((), (), s32[]{:S(2)}) async-start(), calls=%async_computation.4 | async-start | bytes 8650752 | tf_op jit(solution)/shard_map/reduce_scatter | solution.py:40
Sparse Core Ops, SparseCore 0:
  188.6 155.0 reduce-scatter.1
where the time goes:
time: 381 us
  waiting for transfers between devices  191 us (50%)
  blocking collectives  110 us (29%)
  other arithmetic  23.6 us (6%)
  local copies, waits for them, and re-layouts  23.4 us (6%)
  between operations  13.4 us (4%)
  matrix products  12.7 us (3%)
  starting transfers between devices  6.68 us (2%)
    reduce_scatter x1, waiting for transfers between devices, shards(): lax.psum_scatter(contract(got_x, got_dy), 'dp', scatter_dimension=0, tile...  155 us
    all_to_all x1, blocking collectives, shards(): lax.all_to_all(dysend, 'expert', split_axis=0, concat_axis=0, tiled=True)  98.7 us
    all_to_all x1, waiting for transfers between devices, shards(): lax.all_to_all(xsend, 'expert', split_axis=0, concat_axis=0, tiled=True)  35.5 us
    dot_general x1, matrix products, contract(): lax.dot_general(left, right, (((0,), (0,)), ((), ())), preferred_element_...  12.7 us
    all_to_all x1, blocking collectives, shards(): lax.all_to_all(summed.reshape(1, hid // n_dp, ffn), 'expert', split_axis=...  11.3 us
    gather x2, local copies, waits for them, and re-layouts, shards(): x_rows.reshape(nblk, BLOCK, hid)[index]  10.4 us
    unnamed x1, other arithmetic  10.3 us
  transfers between devices with their start and end apart: 2, of which 2 were waited for; matrix products, arithmetic and copies ran while one was open for 3% of the time, Pallas kernels for 0%

commit v1 on v0

--- a/solution.py
+++ b/solution.py
@@ -5,6 +5,12 @@
 
 BLOCK = 128
 CAP = 2
+supply_all_sectors_over_axis = lambda payload: jnp.concatenate(
+    jax.lax.all_to_all(
+        jnp.stack(jnp.split(payload, jax.lax.axis_size("expert"), axis=2)), "expert", 0, 0
+    ),
+    axis=0,
+)
 
 
 def contract(left, right):
@@ -38,9 +44,7 @@
     got_x = got_x.reshape(n_exp * CAP * BLOCK, hid)
     got_dy = got_dy.reshape(n_exp * CAP * BLOCK, ffn)
     summed = lax.psum_scatter(contract(got_x, got_dy), "dp", scatter_dimension=0, tiled=True)
-    return lax.all_to_all(
-        summed.reshape(1, hid // n_dp, ffn), "expert", split_axis=2, concat_axis=0, tiled=True
-    )
+    return supply_all_sectors_over_axis(summed.reshape(1, hid // n_dp, ffn))
 
 
 def solution(mesh):

time: 381 us -> 370 us (0.971)
  other arithmetic: 23.6 us -> 12.1 us
    unnamed x1 -> x0, other arithmetic: 10.3 us -> none
where the time goes in v1:
time: 370 us; the launch traced here: 369 us
  waiting for transfers between devices  191 us (52%)
  blocking collectives  110 us (30%)
  local copies, waits for them, and re-layouts  23.1 us (6%)
  between operations  13.4 us (4%)
  matrix products  12.7 us (3%)
  other arithmetic  12.1 us (3%)
  starting transfers between devices  6.68 us (2%)
    reduce_scatter x1, waiting for transfers between devices, shards(): lax.psum_scatter(contract(got_x, got_dy), 'dp', scatter_dimension=0, tile...  155 us
    all_to_all x1, blocking collectives, shards(): lax.all_to_all(dysend, 'expert', split_axis=0, concat_axis=0, tiled=True)  98.7 us
    all_to_all x1, waiting for transfers between devices, shards(): lax.all_to_all(xsend, 'expert', split_axis=0, concat_axis=0, tiled=True)  35.5 us
    dot_general x1, matrix products, contract(): lax.dot_general(left, right, (((0,), (0,)), ((), ())), preferred_element_...  12.7 us
    all_to_all x1, blocking collectives, jax.lax.all_to_all(jnp.stack(jnp.split(payload, jax.lax.axis_size('expert...  11.3 us
    gather x2, local copies, waits for them, and re-layouts, shards(): x_rows.reshape(nblk, BLOCK, hid)[index]  10.4 us
  transfers between devices with their start and end apart: 2, of which 2 were waited for; matrix products, arithmetic and copies ran while one was open for 3% of the time, Pallas kernels for 0%

profile of v1, /device:TPU:2, one launch (start us, length us, event | category | flops | bytes accessed | tf_op | source)
XLA Modules:
  0.0 368.7 jit_solution(4740482653055925567)
XLA Ops:
  6.5 0.0 copy-start
  6.5 1.0 dynamic-slice_reduce_fusion
  7.6 0.1 iota_compare_fusion
  7.6 0.2 reduce-window.8
  7.8 0.1 add_select_fusion
  7.9 0.1 select_n.41
  8.0 0.1 copy.5
  8.1 0.1 broadcast_bitcast_fusion
  8.2 4.0 %gather_fusion = bf16[16,128,1024]{2,1,0:T(8,128)(2,1)} fusion(bf16[4,128,1024]{2,1,0:T(8,128)(2,1)} %bitcast.54, s32[1024]{0:T(1024)S(1)} %pad_clamp_fusion), kind=kCustom, calls=%fused_computation | custom fusion | bytes 8388672 | tf_op jit(solution)/shard_map/gather | solution.py:36
  12.1 6.5 %copy.6 = bf16[8,256,1024]{1,2,0:T(8,128)(2,1)} copy(bf16[8,256,1024]{2,1,0:T(8,128)(2,1)} %bitcast.53) | data formatting | bytes 8388608 | tf_op jit(solution)/shard_map/gather | solution.py:36
  18.6 4.4 %broadcast_select_fusion = bf16[8,256,1024]{1,2,0:T(8,128)(2,1)} fusion(bf16[8,256,1024]{1,2,0:T(8,128)(2,1)} %copy.6, pred[8,256]{1,0:T(8,128)(4,1)S(1)} %broadcast_bitcast_fusion), kind=kLoop, calls=%fused_computation.4 | loop fusion | flops 2097152 | bytes 8390656 | tf_op jit(solution)/shard_map/jit(_where)/select_n | solution.py:36
  23.0 6.7 %all-to-all-start = ((bf16[8,256,1024]{1,2,0:T(8,128)(2,1)}), bf16[8,256,1024]{1,2,0:T(8,128)(2,1)}, u32[]{:S(2)}, u32[]{:S(2)}) async-start(bf16[8,256,1024]{1,2,0:T(8,128)(2,1)} %broadcast_select_fusion), calls=%async_computation | async-start | bytes 8388608 | tf_op jit(solution)/shard_map/all_to_all | solution.py:41
  29.7 0.0 reduce-scatter.2.cloned.1.call-start
  29.7 0.0 copy-done
  29.7 4.6 %gather_fusion.1 = bf16[16,128,2048]{2,1,0:T(8,128)(2,1)} fusion(bf16[4,128,2048]{2,1,0:T(8,128)(2,1)S(1)} %bitcast.51, s32[1024]{0:T(1024)S(1)} %pad_clamp_fusion), kind=kCustom, calls=%fused_computation.1 | custom fusion | bytes 16777280 | tf_op jit(solution)/shard_map/gather | solution.py:37
  34.3 7.3 %bitcast_select_fusion = bf16[8,256,2048]{2,1,0:T(8,128)(2,1)} fusion(pred[8,256]{1,0:T(8,128)(4,1)S(1)} %broadcast_bitcast_fusion, bf16[8,256,2048]{2,1,0:T(8,128)(2,1)} %bitcast.52), kind=kLoop, calls=%fused_computation.2 | loop fusion | flops 4194304 | bytes 16779264 | tf_op jit(solution)/shard_map/jit(_where)/select_n | solution.py:37
  41.6 35.5 %all-to-all-done = bf16[8,256,1024]{1,2,0:T(8,128)(2,1)} async-done(((bf16[8,256,1024]{1,2,0:T(8,128)(2,1)}), bf16[8,256,1024]{1,2,0:T(8,128)(2,1)}, u32[]{:S(2)}, u32[]{:S(2)}) %all-to-all-start) | async-done | bytes 4194336 | tf_op jit(solution)/shard_map/all_to_all | solution.py:41
  77.0 98.7 %all_to_all.15 = bf16[8,256,2048]{2,1,0:T(8,128)(2,1)S(1)} all-to-all(bf16[8,256,2048]{2,1,0:T(8,128)(2,1)} %bitcast_select_fusion), channel_id=1, replica_groups=mesh['dp'=32,'expert'=8] {'expert'}, dimensions={0} | all-to-all | bytes 16777216 | tf_op jit(solution)/shard_map/all_to_all | solution.py:42
  175.7 12.7 %convolution_bitcast_fusion = f32[1024,2048]{1,0:T(8,128)} fusion(bf16[8,256,1024]{1,2,0:T(8,128)(2,1)} %all-to-all-done, bf16[8,256,2048]{2,1,0:T(8,128)(2,1)S(1)} %all_to_all.15), kind=kOutput, calls=%fused_computation.3 | convolution fusion | flops 8589934592 | bytes 20971520 | tf_op jit(solution)/shard_map/dot_general | solution.py:17
  188.5 0.0 reduce-scatter.2.cloned.1.call-update
  188.5 155.2 %reduce-scatter.2.cloned.1.call-done = f32[32,2048]{1,0:T(8,128)} async-done(((f32[1024,2048]{1,0:T(8,128)}), f32[32,2048]{1,0:T(8,128)}) %reduce-scatter.2.cloned.1.call-update) | async-done | bytes 262160 | tf_op jit(solution)/shard_map/reduce_scatter | solution.py:46
  343.7 0.8 fusion.7
  344.5 0.8 fusion.6
  345.2 0.8 fusion.5
  346.0 0.8 fusion.4
  346.8 0.8 fusion.3
  347.5 0.8 fusion.2
  348.3 0.8 fusion.1
  349.0 0.8 fusion
  349.8 11.3 %all_to_all.16 = f32[8,1,32,256]{3,2,1,0:T(8,128)S(1)} all-to-all(f32[8,1,32,256]{3,2,1,0:T(8,128)S(1)} %fusion), channel_id=1, replica_groups=mesh['dp'=32,'expert'=8] {'expert'}, dimensions={0} | all-to-all | bytes 524288 | tf_op jit(solution)/shard_map/all_to_all | solution.py:9
  361.1 0.7 copy.15
  (3 shorter events, 0.0 us)
Async XLA Ops:
  6.5 23.2 %copy-start = (bf16[512,2048]{1,0:T(8,128)(2,1)S(1)}, bf16[512,2048]{1,0:T(8,128)(2,1)}, u32[]{:S(2)}) copy-start(bf16[512,2048]{1,0:T(8,128)(2,1)} %param.4) | copy-start | bytes 6291460
  23.0 54.0 %all-to-all-start = ((bf16[8,256,1024]{1,2,0:T(8,128)(2,1)}), bf16[8,256,1024]{1,2,0:T(8,128)(2,1)}, u32[]{:S(2)}, u32[]{:S(2)}) async-start(bf16[8,256,1024]{1,2,0:T(8,128)(2,1)} %broadcast_select_fusion), calls=%async_computation | async-start | bytes 8388608 | tf_op jit(solution)/shard_map/all_to_all | solution.py:41
  29.7 314.0 %reduce-scatter.2.cloned.1.call-start = ((), (), s32[]{:S(2)}) async-start(), calls=%async_computation.4 | async-start | bytes 8650752 | tf_op jit(solution)/shard_map/reduce_scatter | solution.py:46
Sparse Core Ops, SparseCore 0:
  188.6 155.0 reduce-scatter.1
